TPU v7x, 32 devices: a whole 2x2x4 slice. The times are simulated.
32 devices in a mesh: ep: 4 (over y, x), fsdp: 8 (over z, core).
Axes of the slice: x: 2, y: 2, z: 4, core: 2. Of those that a mesh axis runs over, the one named last changes fastest.
Arguments:
- train_gate: float32 [128, 2048, 768], P('ep', 'fsdp'), may hold values from -0.1875 to 0.1875
- other_gate: bfloat16 [128, 2048, 768], P('ep', 'fsdp'), may hold values from -0.0625 to 0.0625
- train_up: float32 [128, 2048, 768], P('ep', 'fsdp'), may hold values from -0.1875 to 0.1875
- other_up: bfloat16 [128, 2048, 768], P('ep', 'fsdp'), may hold values from -0.0625 to 0.0625
- router_weight: float32 [2048, 128], P('fsdp', 'ep'), may hold values from -0.125 to 0.125
- router_gain: float32 [2048], P('fsdp'), may hold values from 0.25 to 1.75
Outputs:
- ready_gate: bfloat16 [128, 2048, 768], P(('ep', 'fsdp'))
- ready_up: bfloat16 [128, 2048, 768], P(('ep', 'fsdp'))
- scale_gate: float32 [128, 768], P(('ep', 'fsdp'))
- scale_up: float32 [128, 768], P(('ep', 'fsdp'))
- serve_router: bfloat16 [2048, 128], replicated
All inputs are finite; a program needn't handle non-finite values. Where the computation divides by a largest or mean magnitude, that divisor is 1e-20 or more.
Results may differ from a plain program's by a relative error of at most 0.013.
Values may be sent and summed in bfloat16 or wider, within the bound.
A program may use at most 192 MiB of HBM per device.

v0:
```python
import jax
import jax.numpy as jnp
from jax import lax
from jax.sharding import PartitionSpec as P

D_MODEL = 2048


def shards(train_gate, other_gate, train_up, other_up, router_weight, router_gain):
    latest_gate = train_gate + other_gate.astype(jnp.float32)
    latest_up = train_up + other_up.astype(jnp.float32)
    total_gate, total_up = (
        lax.psum(jnp.sum(jnp.abs(latest_gate), axis=1).astype(jnp.bfloat16), "fsdp").astype(
            jnp.float32
        ),
        lax.psum(jnp.sum(jnp.abs(latest_up), axis=1).astype(jnp.bfloat16), "fsdp").astype(
            jnp.float32
        ),
    )
    scale_gate = total_gate / D_MODEL
    scale_up = total_up / D_MODEL
    narrow_gate, narrow_up = (
        (latest_gate / jnp.expand_dims(scale_gate, 1)).astype(jnp.bfloat16),
        (latest_up / jnp.expand_dims(scale_up, 1)).astype(jnp.bfloat16),
    )
    ready_gate, ready_up = (
        lax.all_to_all(narrow_gate, "fsdp", split_axis=0, concat_axis=1, tiled=True),
        lax.all_to_all(narrow_up, "fsdp", split_axis=0, concat_axis=1, tiled=True),
    )
    scale_gate = lax.dynamic_slice_in_dim(
        scale_gate, lax.axis_index("fsdp") * ready_gate.shape[0], ready_gate.shape[0], axis=0
    )
    scale_up = lax.dynamic_slice_in_dim(
        scale_up, lax.axis_index("fsdp") * ready_up.shape[0], ready_up.shape[0], axis=0
    )
    part_router = (router_weight * router_gain[:, None]).astype(jnp.bfloat16)
    row_router = lax.all_gather(part_router, "fsdp", axis=0, tiled=True)
    serve_router = lax.all_gather(row_router, "ep", axis=1, tiled=True)
    return (ready_gate, ready_up, scale_gate, scale_up, serve_router)


def solution(mesh):
    placed = (
        P("ep", "fsdp", None),
        P("ep", "fsdp", None),
        P("ep", "fsdp", None),
        P("ep", "fsdp", None),
        P("fsdp", "ep"),
        P("fsdp"),
    )
    return jax.shard_map(
        shards,
        mesh=mesh,
        in_specs=placed,
        out_specs=(
            P(("ep", "fsdp"), None, None),
            P(("ep", "fsdp"), None, None),
            P(("ep", "fsdp"), None),
            P(("ep", "fsdp"), None),
            P(),
        ),
        check_vma=False,
    )
```

profile of v0, /device:TPU:0, one launch (start us, length us, event | category | flops | bytes accessed | tf_op | source)
XLA Modules:
  0.0 711.2 jit_solution(16841271009129784802)
XLA Ops:
  7.2 0.0 all-reduce.3.cloned.1.call-start
  7.2 25.2 %abs_reduce_fusion = (bf16[32,768]{1,0:T(8,128)(2,1)}, bf16[32,768]{1,0:T(8,128)(2,1)}) fusion(f32[32,256,768]{2,1,0:T(8,128)} %param.8, bf16[32,256,768]{2,1,0:T(8,128)(2,1)} %param.9, f32[32,256,768]{2,1,0:T(8,128)} %param.6, bf16[32,256,768]{2,1,0:T(8,128)(2,1)} %param.7), kind=kLoop, calls=%fused_computation.1 | loop fusion | flops 50282496 | bytes 75595776 | tf_op jit(solution)/shard_map/reduce_sum | solution.py:16
  32.4 0.0 all-reduce.3.cloned.1.call-update
  32.4 55.4 %all-reduce.3.cloned.1.call-done = (bf16[32,768]{1,0:T(8,128)(2,1)}, bf16[32,768]{1,0:T(8,128)(2,1)}) async-done(((bf16[32,768]{1,0:T(8,128)(2,1)}, bf16[32,768]{1,0:T(8,128)(2,1)}), (bf16[32,768]{1,0:T(8,128)(2,1)}, bf16[32,768]{1,0:T(8,128)(2,1)})) %all-reduce.3.cloned.1.call-update) | async-done | bytes 98320 | tf_op jit(solution)/shard_map/psum | solution.py:13
  87.8 0.8 convert_multiply_fusion.1
  88.6 17.2 %divide_convert_fusion.1 = bf16[32,256,768]{2,1,0:T(8,128)(2,1)} fusion(f32[32,256,768]{2,1,0:T(8,128)} %param.6, bf16[32,256,768]{2,1,0:T(8,128)(2,1)} %param.7, f32[32,768]{1,0:T(8,128)S(1)} %convert_multiply_fusion.1), kind=kLoop, calls=%fused_computation.3 | loop fusion | flops 25165824 | bytes 50429952 | tf_op jit(solution)/shard_map/convert_element_type | solution.py:23
  105.9 0.0 copy-start
  105.9 5.5 all-to-all-start
  111.3 0.0 copy-done
  111.4 17.4 %divide_convert_fusion = bf16[32,256,768]{2,1,0:T(8,128)(2,1)} fusion(f32[32,256,768]{2,1,0:T(8,128)} %param.8, bf16[32,256,768]{2,1,0:T(8,128)(2,1)} %param.9, f32[32,768]{1,0:T(8,128)S(1)} %convert_multiply_fusion), kind=kLoop, calls=%fused_computation | loop fusion | flops 25165824 | bytes 50429952 | tf_op jit(solution)/shard_map/convert_element_type | solution.py:24
  128.7 0.0 copy-start.1
  128.7 0.0 copy-start.2
  128.7 256.4 %all-to-all-done = bf16[32,256,768]{2,1,0:T(8,128)(2,1)} async-done(((bf16[32,256,768]{2,1,0:T(8,128)(2,1)}), bf16[32,256,768]{2,1,0:T(8,128)(2,1)}, u32[]{:S(2)}, u32[]{:S(2)}) %all-to-all-start) | async-done | bytes 12582944 | tf_op jit(solution)/shard_map/all_to_all | solution.py:27
  385.1 5.4 all-to-all-start.1
  390.5 0.0 copy-done.1
  390.5 0.0 copy-done.2
  390.6 280.0 %all_gather.6 = bf16[2048,32]{0,1:T(8,128)(2,1)S(1)} all-gather(bf16[256,32]{0,1:T(8,128)(2,1)S(1)} %multiply_convert_fusion), channel_id=1, replica_groups=mesh['ep'=4,'fsdp'=8] {'fsdp'}, dimensions={0}, use_global_device_ids=true | all-gather | bytes 147456 | tf_op jit(solution)/shard_map/all_gather | solution.py:37
  670.5 10.3 %all_gather.7 = bf16[2048,128]{0,1:T(8,128)(2,1)S(1)} all-gather(bf16[2048,32]{0,1:T(8,128)(2,1)S(1)} %all_gather.6), channel_id=1, replica_groups=mesh['ep'=4,'fsdp'=8] {'ep'}, dimensions={1}, use_global_device_ids=true | all-gather | bytes 655360 | tf_op jit(solution)/shard_map/all_gather | solution.py:38
  680.8 1.0 copy.16
  681.8 0.6 constant_dynamic-slice_fusion
  682.4 0.6 constant_dynamic-slice_fusion.1
  683.0 10.7 %copy.14 = bf16[8,4,256,768]{3,2,0,1:T(8,128)(2,1)} copy(bf16[8,4,256,768]{3,2,1,0:T(8,128)(2,1)} %bitcast) | data formatting | bytes 25165824 | tf_op jit(solution)/shard_map/all_to_all | solution.py:27
  693.7 0.0 all-to-all-done.1
  693.7 10.7 %copy.15 = bf16[8,4,256,768]{3,2,0,1:T(8,128)(2,1)} copy(bf16[8,4,256,768]{3,2,1,0:T(8,128)(2,1)} %bitcast.3) | data formatting | bytes 25165824 | tf_op jit(solution)/shard_map/all_to_all | solution.py:28
  (2 shorter events, 0.0 us)
Async XLA Ops:
  7.2 80.6 %all-reduce.3.cloned.1.call-start = ((), (), s32[]{:S(2)}) async-start(), calls=%async_computation.2 | async-start | bytes 196608 | tf_op jit(solution)/shard_map/psum | solution.py:13
  105.9 5.5 copy-start
  105.9 279.3 %all-to-all-start = ((bf16[32,256,768]{2,1,0:T(8,128)(2,1)}), bf16[32,256,768]{2,1,0:T(8,128)(2,1)}, u32[]{:S(2)}, u32[]{:S(2)}) async-start(bf16[32,256,768]{2,1,0:T(8,128)(2,1)} %divide_convert_fusion.1), calls=%async_computation | async-start | bytes 25165824 | tf_op jit(solution)/shard_map/all_to_all | solution.py:27
  128.7 261.8 %copy-start.1 = (f32[256,32]{0,1:T(8,128)S(1)}, f32[256,32]{0,1:T(8,128)}, u32[]{:S(2)}) copy-start(f32[256,32]{0,1:T(8,128)} %param.10) | copy-start | bytes 98308
  128.7 261.8 %copy-start.2 = (f32[256]{0:T(256)S(1)}, f32[256]{0:T(256)}, u32[]{:S(2)}) copy-start(f32[256]{0:T(256)} %param.11) | copy-start | bytes 3076
  385.1 308.5 %all-to-all-start.1 = ((bf16[32,256,768]{2,1,0:T(8,128)(2,1)}), bf16[32,256,768]{2,1,0:T(8,128)(2,1)}, u32[]{:S(2)}, u32[]{:S(2)}) async-start(bf16[32,256,768]{2,1,0:T(8,128)(2,1)} %divide_convert_fusion), calls=%async_computation.1 | async-start | bytes 25165824 | tf_op jit(solution)/shard_map/all_to_all | solution.py:28
Sparse Core Ops, SparseCore 0:
  32.5 55.2 all-reduce.2
where the time goes:
time: 712 us; the launch traced here: 711 us
  waiting for transfers between devices  312 us (44%)
  blocking collectives  290 us (41%)
  other arithmetic  60.6 us (9%)
  local copies, waits for them, and re-layouts  23.6 us (3%)
  between operations  14.1 us (2%)
  starting transfers between devices  10.9 us (2%)
    all_gather x1, blocking collectives, shards(): row_router = lax.all_gather(part_router, 'fsdp', axis=0, tiled=True)  280 us
    all_to_all x1, waiting for transfers between devices, shards(): lax.all_to_all(narrow_gate, 'fsdp', split_axis=0, concat_axis=1, tiled=True)  256 us
    psum x1, waiting for transfers between devices, shards(): lax.psum(jnp.sum(jnp.abs(latest_gate), axis=1).astype(jnp.bfloat16), 'fsdp')  55.4 us
    reduce_sum x1, other arithmetic, shards(): jnp.sum(jnp.abs(latest_up), axis=1).astype(jnp.bfloat16)  25.2 us
    convert_element_type x1, other arithmetic, shards(): (latest_up / jnp.expand_dims(scale_up, 1)).astype(jnp.bfloat16)  17.4 us
    convert_element_type x1, other arithmetic, shards(): (latest_gate / jnp.expand_dims(scale_gate, 1)).astype(jnp.bfloat16)  17.2 us
  transfers between devices with their start and end apart: 3, of which 2 were waited for; matrix products, arithmetic and copies ran while one was open for 4% of the time, Pallas kernels for 0%

commit v1 on v0

--- a/solution.py
+++ b/solution.py
@@ -10,9 +10,10 @@
     latest_gate = train_gate + other_gate.astype(jnp.float32)
     latest_up = train_up + other_up.astype(jnp.float32)
     total_gate, total_up = (
-        lax.psum(jnp.sum(jnp.abs(latest_gate), axis=1).astype(jnp.bfloat16), "fsdp").astype(
-            jnp.float32
-        ),
+        jnp.sum(
+            lax.all_gather(jnp.sum(jnp.abs(latest_gate), axis=1).astype(jnp.bfloat16), "fsdp"),
+            axis=0,
+        ).astype(jnp.float32),
         lax.psum(jnp.sum(jnp.abs(latest_up), axis=1).astype(jnp.bfloat16), "fsdp").astype(
             jnp.float32
         ),

time: 712 us -> 679 us (0.954)
  waiting for transfers between devices: 312 us -> 0.01 us
  blocking collectives: 290 us -> 582 us
  between operations: 14.1 us -> 0.72 us
    psum x0 -> x1, blocking collectives: none -> 276 us  [shards(): lax.psum(jnp.sum(jnp.abs(latest_up), axis=1).astype(jnp.bfloat16), 'fsdp')]
    all_to_all x1, waiting for transfers between devices: 256 us -> 0.01 us  [shards(): lax.all_to_all(narrow_gate, 'fsdp', split_axis=0, concat_axis=1, tiled=True)]
    psum x1 -> x0, waiting for transfers between devices: 55.4 us -> none  [shards(): lax.psum(jnp.sum(jnp.abs(latest_gate), axis=1).astype(jnp.bfloat16), 'fsdp')]
    all_gather x0 -> x1, blocking collectives: none -> 16.2 us  [shards(): lax.all_gather(jnp.sum(jnp.abs(latest_gate), axis=1).astype(jnp.bfloat16)...]
    reduce_sum x0 -> x2, other arithmetic: none -> 12.9 us  [the longest x1 12.8 us: shards(): jnp.sum(jnp.abs(latest_gate), axis=1).astype(jnp.bfloat16)]
    reduce_sum x1, other arithmetic: 25.2 us -> 12.8 us  [shards(): jnp.sum(jnp.abs(latest_up), axis=1).astype(jnp.bfloat16)]
  transfers between devices with their start and end apart: 3 -> 2, of which waited for: 2 -> 0; matrix products, arithmetic and copies ran while one was open for 4% -> 6% of each run, Pallas kernels for 0% -> 0%
where the time goes in v1:
time: 679 us; the launch traced here: 678 us
  blocking collectives  582 us (86%)
  other arithmetic  60.4 us (9%)
  local copies, waits for them, and re-layouts  23.6 us (3%)
  starting transfers between devices  10.9 us (2%)
    all_gather x1, blocking collectives, shards(): row_router = lax.all_gather(part_router, 'fsdp', axis=0, tiled=True)  280 us
    psum x1, blocking collectives, shards(): lax.psum(jnp.sum(jnp.abs(latest_up), axis=1).astype(jnp.bfloat16), 'fsdp')  276 us
    convert_element_type x1, other arithmetic, shards(): (latest_up / jnp.expand_dims(scale_up, 1)).astype(jnp.bfloat16)  17.4 us
    convert_element_type x1, other arithmetic, shards(): (latest_gate / jnp.expand_dims(scale_gate, 1)).astype(jnp.bfloat16)  17.2 us
    all_gather x1, blocking collectives, shards(): lax.all_gather(jnp.sum(jnp.abs(latest_gate), axis=1).astype(jnp.bfloat16)...  16.2 us
  transfers between devices with their start and end apart: 2, of which 0 were waited for; matrix products, arithmetic and copies ran while one was open for 6% of the time, Pallas kernels for 0%

profile of v1, /device:TPU:0, one launch (start us, length us, event | category | flops | bytes accessed | tf_op | source)
XLA Modules:
  0.0 678.1 jit_solution(15375657672300780454)
XLA Ops:
  0.6 12.8 %abs_reduce_fusion.1 = bf16[32,768]{1,0:T(8,128)(2,1)S(1)} fusion(f32[32,256,768]{2,1,0:T(8,128)} %param.6, bf16[32,256,768]{2,1,0:T(8,128)(2,1)} %param.7), kind=kLoop, calls=%fused_computation.4 | loop fusion | flops 25141248 | bytes 37797888 | tf_op jit(solution)/shard_map/reduce_sum | solution.py:14
  13.5 16.2 %all-gather = bf16[256,768]{1,0:T(8,128)(2,1)S(1)} all-gather(bf16[32,768]{1,0:T(8,128)(2,1)S(1)} %abs_reduce_fusion.1), channel_id=2, replica_groups=mesh['ep'=4,'fsdp'=8] {'fsdp'}, dimensions={0}, use_global_device_ids=true | all-gather | bytes 442368 | tf_op jit(solution)/shard_map/all_gather | solution.py:14
  29.7 0.1 reduce_sum.31
  29.8 17.2 %divide_convert_fusion.1 = bf16[32,256,768]{2,1,0:T(8,128)(2,1)} fusion(f32[32,256,768]{2,1,0:T(8,128)} %param.6, bf16[32,256,768]{2,1,0:T(8,128)(2,1)} %param.7, f32[32,768]{1,0:T(8,128)S(1)} %convert_multiply_fusion.1), kind=kLoop, calls=%fused_computation.3 | loop fusion | flops 25165824 | bytes 50429952 | tf_op jit(solution)/shard_map/convert_element_type | solution.py:24
  47.0 5.3 all-to-all-start
  52.4 12.8 %abs_reduce_fusion = bf16[32,768]{1,0:T(8,128)(2,1)S(1)} fusion(f32[32,256,768]{2,1,0:T(8,128)} %param.8, bf16[32,256,768]{2,1,0:T(8,128)(2,1)} %param.9), kind=kLoop, calls=%fused_computation.1 | loop fusion | flops 25141248 | bytes 37797888 | tf_op jit(solution)/shard_map/reduce_sum | solution.py:17
  65.2 276.0 %psum.7 = bf16[32,768]{1,0:T(8,128)(2,1)S(1)} all-reduce(bf16[32,768]{1,0:T(8,128)(2,1)S(1)} %abs_reduce_fusion), channel_id=1, replica_groups=mesh['ep'=4,'fsdp'=8] {'fsdp'}, use_global_device_ids=true, to_apply=%region_3.0 | all-reduce | flops 24576 | bytes 98304 | tf_op jit(solution)/shard_map/psum | solution.py:17
  341.2 17.4 %divide_convert_fusion = bf16[32,256,768]{2,1,0:T(8,128)(2,1)} fusion(f32[32,256,768]{2,1,0:T(8,128)} %param.8, bf16[32,256,768]{2,1,0:T(8,128)(2,1)} %param.9, f32[32,768]{1,0:T(8,128)S(1)} %convert_multiply_fusion), kind=kLoop, calls=%fused_computation | loop fusion | flops 25165824 | bytes 50429952 | tf_op jit(solution)/shard_map/convert_element_type | solution.py:25
  358.6 0.0 copy-start
  358.6 0.0 copy-start.1
  358.6 0.0 all-to-all-done
  358.7 5.5 all-to-all-start.1
  364.2 0.0 copy-done
  364.2 0.0 copy-done.1
  364.2 280.0 %all_gather.11 = bf16[2048,32]{0,1:T(8,128)(2,1)S(1)} all-gather(bf16[256,32]{0,1:T(8,128)(2,1)S(1)} %multiply_convert_fusion), channel_id=1, replica_groups=mesh['ep'=4,'fsdp'=8] {'fsdp'}, dimensions={0}, use_global_device_ids=true | all-gather | bytes 147456 | tf_op jit(solution)/shard_map/all_gather | solution.py:38
  644.2 10.3 %all_gather.12 = bf16[2048,128]{0,1:T(8,128)(2,1)S(1)} all-gather(bf16[2048,32]{0,1:T(8,128)(2,1)S(1)} %all_gather.11), channel_id=1, replica_groups=mesh['ep'=4,'fsdp'=8] {'ep'}, dimensions={1}, use_global_device_ids=true | all-gather | bytes 655360 | tf_op jit(solution)/shard_map/all_gather | solution.py:39
  654.5 1.0 copy.19
  655.5 0.6 constant_dynamic-slice_fusion.1
  656.1 0.6 constant_dynamic-slice_fusion
  656.7 10.7 %copy.17 = bf16[8,4,256,768]{3,2,0,1:T(8,128)(2,1)} copy(bf16[8,4,256,768]{3,2,1,0:T(8,128)(2,1)} %bitcast.1) | data formatting | bytes 25165824 | tf_op jit(solution)/shard_map/all_to_all | solution.py:28
  667.4 0.0 all-to-all-done.1
  667.4 10.7 %copy.18 = bf16[8,4,256,768]{3,2,0,1:T(8,128)(2,1)} copy(bf16[8,4,256,768]{3,2,1,0:T(8,128)(2,1)} %bitcast.4) | data formatting | bytes 25165824 | tf_op jit(solution)/shard_map/all_to_all | solution.py:29
  (3 shorter events, 0.0 us)
Async XLA Ops:
  47.0 311.6 %all-to-all-start = ((bf16[32,256,768]{2,1,0:T(8,128)(2,1)}), bf16[32,256,768]{2,1,0:T(8,128)(2,1)}, u32[]{:S(2)}, u32[]{:S(2)}) async-start(bf16[32,256,768]{2,1,0:T(8,128)(2,1)} %divide_convert_fusion.1), calls=%async_computation | async-start | bytes 25165824 | tf_op jit(solution)/shard_map/all_to_all | solution.py:28
  358.6 5.6 copy-start
  358.6 5.6 copy-start.1
  358.7 308.7 %all-to-all-start.1 = ((bf16[32,256,768]{2,1,0:T(8,128)(2,1)}), bf16[32,256,768]{2,1,0:T(8,128)(2,1)}, u32[]{:S(2)}, u32[]{:S(2)}) async-start(bf16[32,256,768]{2,1,0:T(8,128)(2,1)} %divide_convert_fusion), calls=%async_computation.1 | async-start | bytes 25165824 | tf_op jit(solution)/shard_map/all_to_all | solution.py:29
